TPU v7x, 128 devices: a whole 4x4x4 slice. The times are simulated.
128 devices in a mesh: expert: 16 (over y, x), mp: 8 (over z, core).
Axes of the slice: x: 4, y: 4, z: 4, core: 2. Of those that a mesh axis runs over, the one named last changes fastest.
Arguments:
- tokens: bfloat16 [2048, 7168], P('expert', 'mp'), may hold values from -0.625 to 0.625
- cotangent: bfloat16 [2048, 8, 2048], P('expert', None, 'mp'), may hold values from -3 to 3
- weights: bfloat16 [32, 7168, 2048], P('expert', 'mp'), may hold values from -0.0625 to 0.0625
- steps: float32 [32, 2048], P('expert', 'mp'), may hold values from 0.002 to 0.02
- expert_ids: int32 [2048, 8], P('expert'), may hold values from 0 to 31, all different within a row; in each aligned block of 128 rows (0 to 127, 128 to 255, ...) at most 64 rows name the same one
Outputs:
- token_grads: bfloat16 [2048, 7168], P('expert', 'mp')
- weight_grads: bfloat16 [32, 7168, 2048], P('expert', 'mp')
- step_grads: float32 [32, 2048], P('expert', 'mp')
Inputs may be any that keep to these rules, and one draw needn't show every extreme that they name: `expert_ids`: each row names 8 different experts; among the 128 rows of one index of the expert axis, no expert is named by more than 64 rows, a bound that some block reaches of them.
All inputs are finite; a program needn't handle non-finite values.
Results may differ from a plain program's by a relative error of at most 0.0058.
Values may be sent and summed in bfloat16 or wider, within the bound.
A program may use at most 128 MiB of HBM per device.

v0:
```python
import functools
import math

import jax
import jax.numpy as jnp
from jax import lax
from jax.experimental import pallas as pl
from jax.experimental.pallas import tpu as pltpu
from jax.sharding import PartitionSpec as P

qmax = 7.0
wiggle = 0.9
two_pi = 6.283185307179586
F32 = jnp.float32
BF16 = jnp.bfloat16

ROOT = math.sqrt(2.0 * wiggle)
SIN = tuple(ROOT * c for c in (3.141592640130707, -5.167710083507862, 2.550077523214134, -0.5982912856178576, 0.0776576603009221))
COS = tuple(
    2.0 * wiggle / (two_pi * qmax * ROOT) * c
    for c in (0.9999999532476082, -4.93479283061961, 4.058411352862034, -1.3318765680776314, 0.2196896110917421)
)


def poly(z, coefs):
    total = coefs[-1] * z + coefs[-2]
    for coef in coefs[-3::-1]:
        total = total * z + coef
    return total


def quantize(w, step7, inv7):
    t = w * inv7
    u = jnp.tanh(t)
    c = qmax * u
    r = c - jnp.round(c)
    z = r * r
    sine = r * poly(z, SIN)
    stair = u - sine * poly(z, COS)
    slopes = ((1.0 - wiggle) + sine * sine) * (1.0 - u * u)
    return step7 * stair, slopes, stair - t * slopes


def dot(a, b, ca, cb):
    return lax.dot_general(a, b, (((ca,), (cb,)), ((), ())), preferred_element_type=F32)


def upper(n):
    rows = lax.broadcasted_iota(jnp.int32, (n, n), 0)
    cols = lax.broadcasted_iota(jnp.int32, (n, n), 1)
    return jnp.where(rows < cols, 1.0, 0.0).astype(BF16)


def slots_of(ids_ref, cap, experts):
    choices, toks = ids_ref.shape
    routes = choices * toks
    expert = lax.broadcasted_iota(jnp.int32, (experts, toks), 0)
    hot = [jnp.where(expert == ids_ref[k : k + 1, :], 1.0, 0.0) for k in range(choices)]
    place = dot(functools.reduce(jnp.add, hot).astype(BF16), upper(toks), 1, 0)
    places = [jnp.sum(one * place, axis=0, keepdims=True) for one in hot]
    both = jnp.concatenate([ids_ref[...].astype(F32), *places], axis=0).astype(BF16)
    token = lax.broadcasted_iota(jnp.int32, (toks, routes), 0)
    route = lax.broadcasted_iota(jnp.int32, (toks, routes), 1)
    spread = dot(both, jnp.where(route // choices == token, 1.0, 0.0).astype(BF16), 1, 0)
    slots = spread[:choices] * float(cap) + spread[choices:]
    choice = lax.broadcasted_iota(jnp.int32, (choices, routes), 0)
    mine = lax.rem(lax.broadcasted_iota(jnp.int32, (choices, routes), 1), choices) == choice
    return jnp.sum(jnp.where(mine, slots, 0.0), axis=0, keepdims=True).astype(jnp.int32)


def selection(ids_ref, first, local, cap):
    groups, _, toks = ids_ref.shape
    ahead = upper(toks)
    picks = []
    for e in range(local):
        named = [jnp.max(jnp.where(ids_ref[i] == first + e, 1.0, 0.0), axis=0, keepdims=True) for i in range(groups)]
        named = jnp.concatenate(named, axis=0)
        place = dot(named.astype(BF16), ahead, 1, 0)
        picks.append(jnp.where(named > 0.0, place, -1.0).astype(jnp.int32))
    return picks


TILE = 128
VMEM_LIMIT = 52 << 20
STEP_COLS = 512
STEP_ROWS = 16


def ring4(pos, device, view, send, recv):
    up, down, far = lax.rem(pos + 1, 4), lax.rem(pos + 3, 4), lax.rem(pos + 2, 4)

    def copy(src, k, part, k_to, n):
        return pltpu.make_async_remote_copy(
            src_ref=view(k, part) if src is None else src,
            dst_ref=view(k, part),
            send_sem=send.at[n],
            recv_sem=recv.at[n],
            device_id=device(k_to),
            device_id_type=pl.DeviceIdType.MESH,
        )

    class Ring:
        def start(self, src=None):
            copy(src, pos, "all", up, 0).start()
            copy(src, pos, "all", down, 1).start()

        def from_down(self):
            copy(None, down, "all", up, 0).wait_recv()
            copy(None, down, "lo", up, 2).start()

        def from_up(self):
            copy(None, up, "all", down, 1).wait_recv()
            copy(None, up, "hi", down, 3).start()

        def finish(self):
            copy(None, far, "lo", up, 2).wait_recv()
            copy(None, far, "hi", down, 3).wait_recv()

        def drain(self):
            copy(None, pos, "all", up, 0).wait_send()
            copy(None, pos, "all", down, 1).wait_send()
            copy(None, down, "lo", up, 2).wait_send()
            copy(None, up, "hi", down, 3).wait_send()

    return Ring()


def all4(pos, device, view, send, recv):
    def copy(k, owner):
        return pltpu.make_async_remote_copy(
            src_ref=view(owner),
            dst_ref=view(owner),
            send_sem=send.at[k],
            recv_sem=recv.at[k],
            device_id=device(lax.rem(pos + k, 4)),
            device_id_type=pl.DeviceIdType.MESH,
        )

    class Direct:
        def start(self):
            for k in (1, 3, 2):
                copy(k, pos).start()

        def finish(self):
            for k in range(1, 4):
                copy(k, lax.rem(pos - k + 4, 4)).wait_recv()

        def drain(self):
            for k in range(1, 4):
                copy(k, pos).wait_send()

    return Direct()


def layer_kernel(
    cap, cot, tokens, ids, steps, weights,
    token_out, weight_out, step_out,
    packed, g, x, ids_all, q, slopes, step_slopes, steps_all, w_buf,
    select, picked, backs, partial, got_1a, got_1b, got_2a, got_2b, sum_a, sum_b, token_t, step_parts, step_got,
    a2a_send, a2a_recv, pair_send, pair_recv, z_send, z_recv, x_send, x_recv,
    s1a_send, s1a_recv, s1b_send, s1b_recv, s2a_send, s2a_recv, s2b_send, s2b_recv,
    ids_send, ids_recv, steps_send, steps_recv, grads_send, grads_recv, own_sem, w_sem,
):
    me, part = lax.axis_index("expert"), lax.axis_index("mp")
    groups, parts = lax.axis_size("expert"), lax.axis_size("mp")
    row, col = me // 4, lax.rem(me, 4)
    z, core = part // 2, lax.rem(part, 2)
    width = cot.shape[-1]
    depth = tokens.shape[1]

    def remote(src, dst, send, recv, expert, mp):
        return pltpu.make_async_remote_copy(
            src_ref=src, dst_ref=dst, send_sem=send, recv_sem=recv,
            device_id=(expert, mp), device_id_type=pl.DeviceIdType.MESH,
        )

    barrier = pltpu.get_barrier_semaphore()
    for k in range(1, groups):
        pl.semaphore_signal(barrier, 1, device_id=(lax.rem(me + k, groups), part), device_id_type=pl.DeviceIdType.MESH)
    for k in range(1, parts):
        pl.semaphore_signal(barrier, 1, device_id=(me, lax.rem(part + k, parts)), device_id_type=pl.DeviceIdType.MESH)
    first_w = pltpu.make_async_copy(weights.at[0, pl.ds(0, TILE), :], w_buf.at[0], w_sem.at[0])
    first_w.start()

    def lanes(p):
        return pl.ds(pl.multiple_of(p * width, width), width)

    own_g = pltpu.make_async_copy(packed.at[me], g.at[:, me, :, lanes(part)], own_sem.at[0])
    own_ids = pltpu.make_async_copy(ids, ids_all.at[me], own_sem.at[2])
    own_steps = pltpu.make_async_copy(steps, steps_all.at[part], own_sem.at[3])
    for own in (own_ids, own_steps):
        own.start()

    x[row, col] = tokens[...].T
    slot_row = slots_of(ids, cap, groups * 2)
    slot = lax.broadcasted_iota(jnp.int32, (2 * cap, slot_row.shape[1]), 0)

    def pack(n, carry):
        to = lax.rem(row - n // 4 + 4, 4) * 4 + lax.rem(col + n, 4)
        pick = jnp.where(slot == slot_row - to * (2 * cap), 1.0, 0.0).astype(BF16)
        packed[to] = dot(pick, cot[...], 1, 0).astype(BF16).reshape(2, cap, width)
        return carry

    pl.semaphore_wait(barrier, groups + parts - 2)

    steps_sent = [
        remote(steps, steps_all.at[part], steps_send.at[k], steps_recv.at[k], me, lax.rem(part + k, parts))
        for k in range(1, parts)
    ]
    for copy in steps_sent:
        copy.start()

    def a2a(r, k):
        to = lax.rem(row - r + 4, 4) * 4 + lax.rem(col + k, 4)
        return remote(packed.at[to], g.at[:, me, :, lanes(part)], a2a_send.at[r, k], a2a_recv.at[r, k], to, part)

    def a2a_wait(r):
        for k in range(4):
            if r or k:
                source = lax.rem(row + r, 4) * 4 + lax.rem(col - k + 4, 4)
                remote(packed.at[source], g.at[:, source, :, lanes(part)], a2a_send.at[r, k], a2a_recv.at[r, k], source, part).wait_recv()

    half = depth // 2

    def on_x(k):
        return (row * 4 + k, part)

    def on_y(k):
        return (k * 4 + col, part)

    def x_pair(piece):
        return pl.ds(2 if piece == "hi" else 0, 4 if piece == "all" else 2)

    x1a = all4(col, on_x, lambda k: x.at[row, k, pl.ds(0, half)], x_send.at[0], x_recv.at[0])
    x1b = all4(row, on_y, lambda k: x.at[k, col, pl.ds(half, half)], x_send.at[1], x_recv.at[1])
    x2a = ring4(row, on_y, lambda k, piece: x.at[k, x_pair(piece), pl.ds(0, half)], x_send.at[2], x_recv.at[2])
    x2b = ring4(col, on_x, lambda k, piece: x.at[x_pair(piece), k, pl.ds(half, half)], x_send.at[3], x_recv.at[3])
    x1a.start()
    x1b.start()
    lax.fori_loop(0, groups // 2, pack, 0)
    own_g.start()
    pairs = [(r, k) for r in range(4) for k in range(4) if r or k]
    for r, k in pairs[:7]:
        a2a(r, k).start()
    ids_sent = [
        remote(ids, ids_all.at[me], ids_send.at[k], ids_recv.at[k], lax.rem(me + k, groups), part) for k in range(1, groups)
    ]
    for copy in ids_sent:
        copy.start()
    lax.fori_loop(groups // 2, groups, pack, 0)
    for r, k in pairs[7:]:
        a2a(r, k).start()

    def on_z(k):
        return (me, k * 2 + core)

    def g_view(r, owner):
        sources = pl.ds(pl.multiple_of(lax.rem(row + r, 4) * 4, 4), 4)

        def view(k, piece):
            some = {"all": pl.ds(0, 2), "lo": pl.ds(0, 1), "hi": pl.ds(1, 1)}[piece]
            return g.at[some, sources, :, lanes(k * 2 + owner)]

        return view

    z_rings = [ring4(z, on_z, g_view(r, core), z_send.at[r], z_recv.at[r]) for r in range(4)]

    def to_pair(r, n):
        view = g_view(r, core)(lax.rem(z + (0, 3, 1, 2)[n], 4), "all")
        return remote(view, view, pair_send.at[r, n], pair_recv.at[r, n], me, z * 2 + 1 - core)

    def from_pair(r, n):
        view = g_view(r, 1 - core)(lax.rem(z + (0, 3, 1, 2)[n], 4), "all")
        return remote(view, view, pair_send.at[r, n], pair_recv.at[r, n], me, z * 2 + 1 - core)

    def arrive(r):
        def event():
            a2a_wait(r)
            if r == 0:
                own_g.wait()
            z_rings[r].start()
            to_pair(r, 0).start()

        return event

    def down(r):
        def event():
            z_rings[r].from_down()
            to_pair(r, 1).start()
            z_rings[r].from_up()
            to_pair(r, 2).start()

        return event

    def far(r):
        def event():
            z_rings[r].finish()
            to_pair(r, 3).start()

        return event

    def x_second():
        for ring, other in ((x1a, x2a), (x1b, x2b)):
            ring.finish()
            other.start()

    def x_mid2():
        for ring in (x2a, x2b):
            ring.from_down()
            ring.from_up()

    tiles_each = weights.shape[1] // TILE
    tiles = weights.shape[0] * tiles_each

    def w_in(t, slot):
        at = pl.ds(pl.multiple_of(lax.rem(t, tiles_each) * TILE, TILE), TILE)
        return pltpu.make_async_copy(weights.at[t // tiles_each, at, :], w_buf.at[slot], w_sem.at[slot])

    def tile(t, carry):
        slot = lax.rem(t, 2)
        w_in(t, slot).wait()

        @pl.when(t + 1 < tiles)
        def _():
            w_in(t + 1, 1 - slot).start()

        e = t // tiles_each
        head = lax.rem(t, tiles_each) * TILE

        def chunk(j, carry):
            cols = pl.ds(pl.multiple_of(j * STEP_COLS, STEP_COLS), STEP_COLS)
            per = STEP_COLS // width
            s = jnp.concatenate([steps_all[j * per + n, pl.ds(e, 1), :] for n in range(per)], axis=1)
            step7 = qmax * s
            inv7 = 1.0 / step7

            def rows(k, carry):
                at = pl.ds(pl.multiple_of(k * STEP_ROWS, STEP_ROWS), STEP_ROWS)
                to = pl.ds(pl.multiple_of(head + k * STEP_ROWS, STEP_ROWS), STEP_ROWS)
                level, slope, step_slope = quantize(w_buf[slot, at, cols].astype(F32), step7, inv7)
                q[e, to, cols] = level.astype(BF16)
                slopes[e, to, cols] = slope.astype(BF16)
                step_slopes[e, to, cols] = step_slope.astype(BF16)
                return carry

            return lax.fori_loop(0, TILE // STEP_ROWS, rows, carry, unroll=2)

        lax.fori_loop(0, weights.shape[2] // STEP_COLS, chunk, 0)
        return carry

    top = sum_a.shape[1]
    bottom = depth - top

    def block_rows(r):
        return pl.multiple_of(lax.rem(row + r, 4) * 4, 4)

    def arrived(r):
        for n in range(4):
            from_pair(r, n).wait_recv()

    def selections():
        own_ids.wait()
        for copy in ids_sent:
            copy.wait_recv()
        places = selection(ids_all, me * 2, 2, cap)
        slot = lax.broadcasted_iota(jnp.int32, (2 * cap, 2 * ids.shape[1]), 0)
        for e in range(2):
            for n in range(groups // 2):
                first, second = places[e][2 * n : 2 * n + 1], places[e][2 * n + 1 : 2 * n + 2]
                place = jnp.concatenate([first, jnp.where(second < 0, second, second + cap)], axis=1)
                select[n, pl.ds(e * 2 * cap, 2 * cap)] = jnp.where(slot == place, 1.0, 0.0).astype(BF16)

    def picks():
        def one(n, carry):
            both = jnp.concatenate([x[n // 2, 2 * lax.rem(n, 2)], x[n // 2, 2 * lax.rem(n, 2) + 1]], axis=1)
            out = dot(both, select[n], 1, 1).astype(BF16)
            at = pl.ds(pl.multiple_of(n * 2 * cap, 2 * cap), 2 * cap)
            for e in range(2):
                picked[e, :, at] = out[:, 2 * cap * e : 2 * cap * (e + 1)]
            return carry

        lax.fori_loop(0, groups // 2, one, 0)

    def back(r):
        base = block_rows(r)
        for e in range(2):
            backs[e] = dot(q[e], g[e, pl.ds(base, 4)].reshape(4 * cap, -1), 1, 1).astype(BF16)
        for n in range(2):
            both = jnp.concatenate([backs[e, :, 2 * cap * n : 2 * cap * (n + 1)] for e in range(2)], axis=1)
            out = dot(both, select[base // 2 + n], 1, 0).astype(BF16)
            for k in range(2):
                partial[r, 2 * n + k] = out[:, 2 * cap * k : 2 * cap * (k + 1)]

    def s1a(r, k):
        to = lax.rem(col + k, 4)
        return remote(
            partial.at[r, to, pl.ds(0, top)], got_1a.at[r, k - 1], s1a_send.at[r, k], s1a_recv.at[r, k], row * 4 + to, part
        )

    def s1b(r):
        to = lax.rem(row + r, 4)
        return remote(
            partial.at[r, :, pl.ds(top, bottom)], got_1b.at[r - 1], s1b_send.at[r], s1b_recv.at[r], to * 4 + col, part
        )

    def s2a(r):
        to = lax.rem(row + r, 4)
        return remote(sum_a.at[r - 1], got_2a.at[r - 1], s2a_send.at[r], s2a_recv.at[r], to * 4 + col, part)

    def s2b(k):
        to = lax.rem(col + k, 4)
        return remote(sum_b.at[k - 1], got_2b.at[k - 1], s2b_send.at[k], s2b_recv.at[k], row * 4 + to, part)

    def send_first(r):
        for k in range(1, 4):
            s1a(r, k).start()
        if r:
            s1b(r).start()

    def upper_sum(r):
        for k in range(1, 4):
            s1a(r, k).wait_recv()
        total = partial[r, col, pl.ds(0, top)].astype(F32)
        for k in range(3):
            total = total + got_1a[r, k].astype(F32)
        return total

    def second_a(r):
        sum_a[r - 1] = upper_sum(r).astype(BF16)

    def lower_sum(k):
        to = lax.rem(col + k, 4)
        total = partial[0, to, pl.ds(top, bottom)].astype(F32)
        for r in range(3):
            total = total + got_1b[r, to].astype(F32)
        return total

    def second_b():
        for r in range(1, 4):
            s1b(r).wait_recv()
        for k in range(1, 4):
            sum_b[k - 1] = lower_sum(k).astype(BF16)

    def grads(k):
        to = lax.rem(part + k, parts)
        return remote(step_parts.at[to], step_got.at[k - 1], grads_send.at[k], grads_recv.at[k], me, to)

    def raw(n, carry):
        p = lax.rem(part + 1 + n, parts)
        cols = lanes(p)

        for e in range(2):
            value = dot(picked[e], g[e, :, :, cols].reshape(groups * cap, width), 1, 0)
            weight_out[e, :, cols] = (value * slopes[e, :, cols].astype(F32)).astype(BF16)
            step_parts[p, pl.ds(e, 1), :] = jnp.sum(value * step_slopes[e, :, cols].astype(F32), axis=0, keepdims=True)
        @pl.when(n > 0)
        def _():
            grads(n).start()

        return carry

    own_steps.wait()
    for copy in steps_sent:
        copy.wait_recv()

    plan = (
        (2, x_second), (4, arrive(0)), (6, arrive(1)), (9, down(0)), (10, arrive(2)), (12, down(1)), (12, arrive(3)),
    )
    done = 0
    for until, event in plan:
        if until > done:
            lax.fori_loop(done, until, tile, 0)
            done = until
        event()
    lax.fori_loop(done, tiles, tile, 0)

    selections()
    far(0)()
    x_mid2()
    arrived(0)
    back(0)
    send_first(0)
    down(2)()
    far(1)()
    arrived(1)
    back(1)
    send_first(1)
    for ring in (x2a, x2b):
        ring.finish()
    down(3)()
    picks()
    far(2)()
    arrived(2)
    back(2)
    send_first(2)
    far(3)()
    arrived(3)
    back(3)
    send_first(3)
    second_a(1)
    lax.fori_loop(0, 1, raw, 0)
    s2a(1).start()
    lax.fori_loop(1, 5, raw, 0)
    second_a(2)
    lax.fori_loop(5, 6, raw, 0)
    s2a(2).start()
    lax.fori_loop(6, parts, raw, 0)
    second_a(3)
    s2a(3).start()
    second_b()
    upper = upper_sum(0)
    for k in range(1, 4):
        s2b(k).start()
    for r in range(1, 4):
        s2a(r).wait_recv()
        upper = upper + got_2a[r - 1].astype(F32)
    token_t[pl.ds(0, top)] = upper.astype(BF16)
    total = lower_sum(0)
    for k in range(1, 4):
        s2b(k).wait_recv()
        total = total + got_2b[k - 1].astype(F32)
    token_t[pl.ds(top, bottom)] = total.astype(BF16)
    token_out[...] = token_t[...].T
    total = step_parts[part]
    for k in range(1, parts):
        grads(k).wait_recv()
        total = total + step_got[k - 1]
    step_out[...] = total * (qmax / math.sqrt(depth * parts * qmax))

    for copy in steps_sent + ids_sent:
        copy.wait_send()
    for r, k in pairs:
        a2a(r, k).wait_send()
    for ring in (x1a, x1b, x2a, x2b, *z_rings):
        ring.drain()
    for r in range(4):
        for n in range(4):
            to_pair(r, n).wait_send()
    for k in range(1, 4):
        for r in range(4):
            s1a(r, k).wait_send()
        s1b(k).wait_send()
        s2a(k).wait_send()
        s2b(k).wait_send()
    for k in range(1, parts):
        grads(k).wait_send()


def layer(cot, tokens, ids, steps, weights):
    groups, parts = lax.axis_size("expert"), lax.axis_size("mp")
    e, d, f = weights.shape
    toks, width = tokens.shape
    cap, part_f = toks // 2, cot.shape[1]
    top = d * 5 // 8 // 16 * 16
    bottom = d - top
    dma = pltpu.SemaphoreType.DMA
    vmem = pl.BlockSpec(memory_space=pltpu.VMEM)
    anywhere = pl.BlockSpec(memory_space=pl.ANY)
    slots = e * cap

    def room(*shape, dtype=BF16):
        return pltpu.VMEM(shape, dtype)

    return pl.pallas_call(
        functools.partial(layer_kernel, cap),
        in_specs=[vmem] * 4 + [anywhere],
        out_specs=[vmem, vmem, vmem],
        out_shape=[
            pltpu.VMEM((toks, width), BF16),
            pltpu.VMEM((e, d, f), BF16),
            pltpu.VMEM((e, part_f), F32),
        ],
        scratch_shapes=[
            room(groups, e, cap, part_f),
            room(e, groups, cap, f),
            room(4, groups // 4, d, toks),
            room(groups, *ids.shape, dtype=jnp.int32),
            room(e, d, f), room(e, d, f), room(e, d, f),
            room(parts, *steps.shape, dtype=F32),
            room(2, TILE, f),
            room(groups // 2, 2 * slots, 2 * toks),
            room(e, d, groups * cap),
            room(e, d, 4 * cap),
            room(4, 4, d, toks),
            room(4, 3, top, toks),
            room(3, 4, bottom, toks),
            room(3, top, toks), room(3, bottom, toks), room(3, top, toks), room(3, bottom, toks),
            room(d, toks),
            room(parts, e, part_f, dtype=F32),
            room(parts - 1, e, part_f, dtype=F32),
            *[dma((4, 4))] * 8,
            *[dma((4, 4))] * 2, *[dma((4,))] * 6,
            dma((groups,)), dma((groups,)), dma((parts,)), dma((parts,)), dma((parts,)), dma((parts,)),
            dma((4,)), dma((2,)),
        ],
        compiler_params=pltpu.CompilerParams(collective_id=0, has_side_effects=True, vmem_limit_bytes=VMEM_LIMIT),
        name="layer",
    )(cot, tokens, ids, steps, weights)


def per_device(tokens, cotangent, weights, steps, expert_ids):
    toks, top_k = expert_ids.shape
    cot = cotangent.reshape(toks * top_k, cotangent.shape[2])
    return tuple(layer(cot, tokens, expert_ids.T, steps, weights))


def solution(mesh):
    return jax.shard_map(
        per_device,
        mesh=mesh,
        in_specs=(
            P("expert", "mp"),
            P("expert", None, "mp"),
            P("expert", "mp", None),
            P("expert", "mp"),
            P("expert", None),
        ),
        out_specs=(P("expert", "mp"), P("expert", "mp", None), P("expert", "mp")),
        check_vma=False,
    )
```

profile of v0, /device:TPU:1, one launch (start us, length us, event | category | flops | bytes accessed | tf_op | source)
XLA Modules:
  0.0 88.0 jit_solution(15776776703163503293)
XLA Ops:
  0.6 83.0 %layer.1 = (bf16[128,896]{1,0:T(8,128)(2,1)S(1)}, bf16[2,896,2048]{2,1,0:T(8,128)(2,1)S(1)}, f32[2,256]{1,0:T(2,128)S(1)}) custom-call(bf16[1024,256]{1,0:T(8,128)(2,1)} %bitcast.2, bf16[128,896]{1,0:T(8,128)(2,1)} %tokens.1, s32[8,128]{1,0:T(8,128)} %bitcast.3, f32[2,256]{1,0:T(2,128)} %steps.1, bf16[2,896,2048]{2,1,0:T(8,128)(2,1)} %weights.1), custom_call_target="tpu_custom_call" | custom-call | tf_op jit(solution)/shard_map/layer/pallas_call | solution.py:564
  83.6 0.7 copy.11
  84.3 0.6 copy.13
  84.9 3.0 %copy.12 = bf16[2,896,2048]{2,1,0:T(8,128)(2,1)} copy(bf16[2,896,2048]{2,1,0:T(8,128)(2,1)S(1)} %get-tuple-element.4) | data formatting | bytes 14680064
where the time goes:
time: 88.1 us; the launch traced here: 88 us
  Pallas kernels  83 us (94%)
  local copies, waits for them, and re-layouts  4.32 us (5%)
    pallas_call x1, Pallas kernels, layer(): pl.pallas_call(functools.partial(layer_kernel, cap), in_specs=[vmem] * 4...  83 us
    unnamed x3, local copies, waits for them, and re-layouts  4.32 us

commit v1 on v0

--- a/solution.py
+++ b/solution.py
@@ -391,10 +391,18 @@
             for k in range(2):
                 partial[r, 2 * n + k] = out[:, 2 * cap * k : 2 * cap * (k + 1)]
 
-    def s1a(r, k):
+    cut = top // 32 * 16
+
+    def piece(r, c):
+        if r < 3:
+            return pl.ds(0, top)
+        return pl.ds(cut, top - cut) if c else pl.ds(0, cut)
+
+    def s1a(r, k, c=0):
         to = lax.rem(col + k, 4)
         return remote(
-            partial.at[r, to, pl.ds(0, top)], got_1a.at[r, k - 1], s1a_send.at[r, k], s1a_recv.at[r, k], row * 4 + to, part
+            partial.at[r, to, piece(r, c)], got_1a.at[r, k - 1, piece(r, c)], s1a_send.at[r + c, k], s1a_recv.at[r + c, k],
+            row * 4 + to, part,
         )
 
     def s1b(r):
@@ -403,30 +411,34 @@
             partial.at[r, :, pl.ds(top, bottom)], got_1b.at[r - 1], s1b_send.at[r], s1b_recv.at[r], to * 4 + col, part
         )
 
-    def s2a(r):
+    def s2a(r, c=0):
         to = lax.rem(row + r, 4)
-        return remote(sum_a.at[r - 1], got_2a.at[r - 1], s2a_send.at[r], s2a_recv.at[r], to * 4 + col, part)
+        n = 0 if c else r
+        return remote(
+            sum_a.at[r - 1, piece(r, c)], got_2a.at[r - 1, piece(r, c)], s2a_send.at[n], s2a_recv.at[n], to * 4 + col, part
+        )
 
     def s2b(k):
         to = lax.rem(col + k, 4)
         return remote(sum_b.at[k - 1], got_2b.at[k - 1], s2b_send.at[k], s2b_recv.at[k], row * 4 + to, part)
 
     def send_first(r):
-        for k in range(1, 4):
-            s1a(r, k).start()
+        for c in range(2 if r == 3 else 1):
+            for k in range(1, 4):
+                s1a(r, k, c).start()
         if r:
             s1b(r).start()
 
-    def upper_sum(r):
+    def upper_sum(r, c=0):
         for k in range(1, 4):
-            s1a(r, k).wait_recv()
-        total = partial[r, col, pl.ds(0, top)].astype(F32)
+            s1a(r, k, c).wait_recv()
+        total = partial[r, col, piece(r, c)].astype(F32)
         for k in range(3):
-            total = total + got_1a[r, k].astype(F32)
+            total = total + got_1a[r, k, piece(r, c)].astype(F32)
         return total
 
-    def second_a(r):
-        sum_a[r - 1] = upper_sum(r).astype(BF16)
+    def second_a(r, c=0):
+        sum_a[r - 1, piece(r, c)] = upper_sum(r, c).astype(BF16)
 
     def lower_sum(k):
         to = lax.rem(col + k, 4)
@@ -464,7 +476,7 @@
         copy.wait_recv()
 
     plan = (
-        (2, x_second), (4, arrive(0)), (6, arrive(1)), (9, down(0)), (10, arrive(2)), (12, down(1)), (12, arrive(3)),
+        (2, x_second), (3, arrive(0)), (6, arrive(1)), (8, down(0)), (9, arrive(2)), (11, down(1)), (12, arrive(3)),
     )
     done = 0
     for until, event in plan:
@@ -500,26 +512,30 @@
     second_a(1)
     lax.fori_loop(0, 1, raw, 0)
     s2a(1).start()
-    lax.fori_loop(1, 5, raw, 0)
+    lax.fori_loop(1, 4, raw, 0)
     second_a(2)
-    lax.fori_loop(5, 6, raw, 0)
+    lax.fori_loop(4, 5, raw, 0)
     s2a(2).start()
-    lax.fori_loop(6, parts, raw, 0)
+    lax.fori_loop(5, 7, raw, 0)
     second_a(3)
+    lax.fori_loop(7, parts, raw, 0)
     s2a(3).start()
     second_b()
-    upper = upper_sum(0)
+    lower = lower_sum(0)
     for k in range(1, 4):
         s2b(k).start()
+    second_a(3, 1)
+    upper = upper_sum(0)
+    s2a(3, 1).start()
+    s2a(3, 1).wait_recv()
     for r in range(1, 4):
         s2a(r).wait_recv()
         upper = upper + got_2a[r - 1].astype(F32)
     token_t[pl.ds(0, top)] = upper.astype(BF16)
-    total = lower_sum(0)
     for k in range(1, 4):
         s2b(k).wait_recv()
-        total = total + got_2b[k - 1].astype(F32)
-    token_t[pl.ds(top, bottom)] = total.astype(BF16)
+        lower = lower + got_2b[k - 1].astype(F32)
+    token_t[pl.ds(top, bottom)] = lower.astype(BF16)
     token_out[...] = token_t[...].T
     total = step_parts[part]
     for k in range(1, parts):
@@ -538,9 +554,12 @@
             to_pair(r, n).wait_send()
     for k in range(1, 4):
         for r in range(4):
-            s1a(r, k).wait_send()
+            for c in range(2 if r == 3 else 1):
+                s1a(r, k, c).wait_send()
         s1b(k).wait_send()
         s2a(k).wait_send()
+        if k == 3:
+            s2a(k, 1).wait_send()
         s2b(k).wait_send()
     for k in range(1, parts):
         grads(k).wait_send()
@@ -551,7 +570,7 @@
     e, d, f = weights.shape
     toks, width = tokens.shape
     cap, part_f = toks // 2, cot.shape[1]
-    top = d * 5 // 8 // 16 * 16
+    top = d * 5 // 7 // 16 * 16
     bottom = d - top
     dma = pltpu.SemaphoreType.DMA
     vmem = pl.BlockSpec(memory_space=pltpu.VMEM)
@@ -589,7 +608,7 @@
             room(parts, e, part_f, dtype=F32),
             room(parts - 1, e, part_f, dtype=F32),
             *[dma((4, 4))] * 8,
-            *[dma((4, 4))] * 2, *[dma((4,))] * 6,
+            *[dma((5, 4))] * 2, *[dma((4,))] * 6,
             dma((groups,)), dma((groups,)), dma((parts,)), dma((parts,)), dma((parts,)), dma((parts,)),
             dma((4,)), dma((2,)),
         ],

time: 88.1 us -> 86.5 us (0.982)
  Pallas kernels: 83 us -> 81.4 us
    pallas_call x1, Pallas kernels: 83 us -> 81.4 us  [layer(): pl.pallas_call(functools.partial(layer_kernel, cap), in_specs=[vmem] * 4...]
where the time goes in v1:
time: 86.5 us; the launch traced here: 86.4 us
  Pallas kernels  81.4 us (94%)
  local copies, waits for them, and re-layouts  4.32 us (5%)
    pallas_call x1, Pallas kernels, layer(): pl.pallas_call(functools.partial(layer_kernel, cap), in_specs=[vmem] * 4...  81.4 us
    unnamed x3, local copies, waits for them, and re-layouts  4.32 us

profile of v1, /device:TPU:1, one launch (start us, length us, event | category | flops | bytes accessed | tf_op | source)
XLA Modules:
  0.0 86.4 jit_solution(4770636259358570573)
XLA Ops:
  0.6 81.4 %layer.1 = (bf16[128,896]{1,0:T(8,128)(2,1)S(1)}, bf16[2,896,2048]{2,1,0:T(8,128)(2,1)S(1)}, f32[2,256]{1,0:T(2,128)S(1)}) custom-call(bf16[1024,256]{1,0:T(8,128)(2,1)} %bitcast.2, bf16[128,896]{1,0:T(8,128)(2,1)} %tokens.1, s32[8,128]{1,0:T(8,128)} %bitcast.3, f32[2,256]{1,0:T(2,128)} %steps.1, bf16[2,896,2048]{2,1,0:T(8,128)(2,1)} %weights.1), custom_call_target="tpu_custom_call" | custom-call | tf_op jit(solution)/shard_map/layer/pallas_call | solution.py:583
  82.1 0.7 copy.11
  82.7 0.6 copy.13
  83.3 3.0 %copy.12 = bf16[2,896,2048]{2,1,0:T(8,128)(2,1)} copy(bf16[2,896,2048]{2,1,0:T(8,128)(2,1)S(1)} %get-tuple-element.4) | data formatting | bytes 14680064

commit v2 on v1

--- a/solution.py
+++ b/solution.py
@@ -424,7 +424,7 @@
 
     def send_first(r):
         for c in range(2 if r == 3 else 1):
-            for k in range(1, 4):
+            for k in (1, 3, 2):
                 s1a(r, k, c).start()
         if r:
             s1b(r).start()

time: 86.5 us -> 86.7 us (level)
  no operation moved by 1% of the time
where the time goes in v2:
time: 86.7 us; the launch traced here: 86.6 us
  Pallas kernels  81.6 us (94%)
  local copies, waits for them, and re-layouts  4.32 us (5%)
    pallas_call x1, Pallas kernels, layer(): pl.pallas_call(functools.partial(layer_kernel, cap), in_specs=[vmem] * 4...  81.6 us
    unnamed x3, local copies, waits for them, and re-layouts  4.32 us

profile of v2, /device:TPU:1, one launch (start us, length us, event | category | flops | bytes accessed | tf_op | source)
XLA Modules:
  0.0 86.6 jit_solution(6550377341060025751)
XLA Ops:
  0.6 81.6 %layer.1 = (bf16[128,896]{1,0:T(8,128)(2,1)S(1)}, bf16[2,896,2048]{2,1,0:T(8,128)(2,1)S(1)}, f32[2,256]{1,0:T(2,128)S(1)}) custom-call(bf16[1024,256]{1,0:T(8,128)(2,1)} %bitcast.2, bf16[128,896]{1,0:T(8,128)(2,1)} %tokens.1, s32[8,128]{1,0:T(8,128)} %bitcast.3, f32[2,256]{1,0:T(2,128)} %steps.1, bf16[2,896,2048]{2,1,0:T(8,128)(2,1)} %weights.1), custom_call_target="tpu_custom_call" | custom-call | tf_op jit(solution)/shard_map/layer/pallas_call | solution.py:583
  82.2 0.7 copy.11
  82.9 0.6 copy.13
  83.5 3.0 %copy.12 = bf16[2,896,2048]{2,1,0:T(8,128)(2,1)} copy(bf16[2,896,2048]{2,1,0:T(8,128)(2,1)S(1)} %get-tuple-element.4) | data formatting | bytes 14680064
